TPU v7x, 32 devices: a whole 2x2x4 slice. The times are simulated.
32 devices in a mesh: dp: 8 (over z, y), mp: 4 (over x, core).
Axes of the slice: x: 2, y: 2, z: 4, core: 2. Of those that a mesh axis runs over, the one named last changes fastest.
Arguments:
- pixels: bfloat16 [20480, 1280], P(('dp', 'mp')), may hold values from -6 to 6
- embed_weight: bfloat16 [4, 1280, 1024], P(None, None, 'mp'), may hold values from -0.15625 to 0.15625
- embed_bias: bfloat16 [4, 1024], replicated, may hold values from -3 to 3
- first_gain: float32 [1024], replicated, may hold values from 0.5 to 1.5
- first_shift: float32 [1024], replicated, may hold values from -1.75 to 1.75
- query_weight: bfloat16 [1024, 1024], P(None, 'mp'), may hold values from -0.1875 to 0.1875
- query_bias: bfloat16 [1024], P('mp'), may hold values from -1.75 to 1.75
- key_weight: bfloat16 [1024, 1024], P(None, 'mp'), may hold values from -0.1875 to 0.1875
- value_weight: bfloat16 [1024, 1024], P(None, 'mp'), may hold values from -0.1875 to 0.1875
- value_bias: bfloat16 [1024], P('mp'), may hold values from -1.75 to 1.75
- output_weight: bfloat16 [1024, 1024], P('mp'), may hold values from -3 to 3
- output_bias: bfloat16 [1024], replicated, may hold values from -1.75 to 1.75
- second_gain: float32 [1024], replicated, may hold values from 0.5 to 1.5
- second_shift: float32 [1024], replicated, may hold values from -1.75 to 1.75
- up_weight: bfloat16 [1024, 4096], P(None, 'mp'), may hold values from -0.1875 to 0.1875
- up_bias: bfloat16 [4096], P('mp'), may hold values from -1.75 to 1.75
- down_weight: bfloat16 [4096, 1024], P('mp'), may hold values from -0.09375 to 0.09375
- down_bias: bfloat16 [1024], replicated, may hold values from -1.75 to 1.75
- cotangent: bfloat16 [20480, 1024], P(('dp', 'mp')), may hold values from -6 to 6
- item_lengths: int32 [8, 5], P('dp'), may hold values from 1 to 588, 2520 in all within a row
- item_kind: int32 [8, 5], P('dp'), may hold values from 0 to 1
- sampling_level: int32 [8, 5], P('dp'), may hold values from 0 to 7
Outputs:
- layer_output: bfloat16 [20480, 1024], P(('dp', 'mp'))
- pixel_gradient: float32 [20480, 1280], P(('dp', 'mp'))
- embed_weight_gradient: float32 [4, 1280, 1024], P(None, None, 'mp')
- embed_bias_gradient: float32 [4, 1024], replicated
- first_gain_gradient: float32 [1024], replicated
- first_shift_gradient: float32 [1024], replicated
- query_weight_gradient: float32 [1024, 1024], P(None, 'mp')
- query_bias_gradient: float32 [1024], P('mp')
- key_weight_gradient: float32 [1024, 1024], P(None, 'mp')
- value_weight_gradient: float32 [1024, 1024], P(None, 'mp')
- value_bias_gradient: float32 [1024], P('mp')
- output_weight_gradient: float32 [1024, 1024], P('mp')
- output_bias_gradient: float32 [1024], replicated
- second_gain_gradient: float32 [1024], replicated
- second_shift_gradient: float32 [1024], replicated
- up_weight_gradient: float32 [1024, 4096], P(None, 'mp')
- up_bias_gradient: float32 [4096], P('mp')
- down_weight_gradient: float32 [4096, 1024], P('mp')
- down_bias_gradient: float32 [1024], replicated
Inputs may be any that keep to these rules, and one draw needn't show every extreme that they name: `item_lengths`: in each group the 5 lengths add up to 2520, the largest is 588; the rows after the items are padding.
All inputs are finite; a program needn't handle non-finite values.
Results may differ from a plain program's by a relative error of at most 0.02.
Values may be sent and summed in bfloat16 or wider, within the bound.
A program may use at most 320 MiB of HBM per device.

v0:
```python
import math

import jax
import jax.numpy as jnp
from jax import lax
from jax.sharding import PartitionSpec as P

HD = 64
GRID = 14
QB = 512
ITEM_MAX = 588


HIGHEST_PRECISION = lax.Precision.HIGHEST
INV_ROOT_TWO = 1.0 / math.sqrt(2.0)
INV_ROOT_TAU = 1.0 / math.sqrt(2.0 * math.pi)


def row_tables(lengths, kinds, levels, row_number, used_rows, grid_side):
    ends = jnp.cumsum(lengths, dtype=jnp.int32)
    starts = ends - lengths
    segment = jnp.sum(
        (row_number[:, None] >= ends[None, :]).astype(jnp.int32), axis=1, dtype=jnp.int32
    )
    starts_all = jnp.concatenate([starts, jnp.full((1,), used_rows, jnp.int32)])
    kinds_all = jnp.concatenate([kinds, jnp.ones((1,), jnp.int32)])
    levels_all = jnp.concatenate([levels, jnp.zeros((1,), jnp.int32)])
    selector = segment[:, None] == jnp.arange(lengths.shape[0] + 1, dtype=jnp.int32)[None, :]
    row_begin = jnp.sum(jnp.where(selector, starts_all[None, :], 0), axis=1, dtype=jnp.int32)
    row_kind = jnp.sum(jnp.where(selector, kinds_all[None, :], 0), axis=1, dtype=jnp.int32)
    row_level = jnp.sum(jnp.where(selector, levels_all[None, :], 0), axis=1, dtype=jnp.int32)
    offset = row_number - row_begin
    band = jnp.where(row_kind == 0, offset // (grid_side * grid_side) % 3, 3)
    return (segment, offset, band, row_level)


def position_code(offset, level, model_width, grid_side):
    quarter = model_width // 4
    cell = offset % (grid_side * grid_side)
    row_place = (cell // grid_side).astype(jnp.float32)
    col_place = (cell % grid_side).astype(jnp.float32)
    scale = jnp.exp2(level.astype(jnp.float32) * 0.5 - 1.5)
    freq = jnp.exp(jnp.arange(quarter).astype(jnp.float32) * (-math.log(10000.0) / quarter))
    row_angle = (row_place * scale)[:, None] * freq[None, :]
    col_angle = (col_place * scale)[:, None] * freq[None, :]
    return jnp.concatenate(
        [jnp.sin(row_angle), jnp.cos(row_angle), jnp.sin(col_angle), jnp.cos(col_angle)], axis=1
    )


def norm_parts(values, gain, shift):
    center = jnp.mean(values, axis=-1, keepdims=True)
    centered = values - center
    spread = jnp.mean(centered * centered, axis=-1, keepdims=True)
    inverse = lax.rsqrt(spread + 1e-06)
    scaled = centered * inverse
    return ((scaled * gain + shift).astype(jnp.bfloat16), scaled, inverse)


def norm_back(grad_rows, scaled, inverse, gain):
    weighted = grad_rows * gain
    return inverse * (
        weighted
        - jnp.mean(weighted, axis=-1, keepdims=True)
        - scaled * jnp.mean(weighted * scaled, axis=-1, keepdims=True)
    )


def gelu_slope(hidden):
    return (
        0.5 * (1.0 + lax.erf(hidden * INV_ROOT_TWO))
        + hidden * jnp.exp(-0.5 * hidden * hidden) * INV_ROOT_TAU
    )


def block_window(block_index, total_rows):
    query_start = block_index * QB
    key_start = jnp.clip(query_start - 2 * QB, 0, total_rows - 5 * QB)
    return (query_start, key_start)


def segment_scores(query_block, key_block, query_segment, key_segment):
    allowed = (query_segment[:, None] == key_segment[None, :])[None]
    scores = (
        jnp.einsum("qhd,khd->hqk", query_block, key_block, preferred_element_type=jnp.float32)
        * 0.125
    )
    return jnp.where(allowed, scores, -1e30)


def masked_scores(query_block, key_block, segment, query_start, key_start):
    query_segment = lax.dynamic_slice_in_dim(segment, query_start, QB, 0)
    key_segment = lax.dynamic_slice_in_dim(segment, key_start, 5 * QB, 0)
    return segment_scores(query_block, key_block, query_segment, key_segment)


def attention_forward(query, keys, values, segment):
    total_rows = query.shape[0]

    def one_block(block_index):
        query_start, key_start = block_window(block_index, total_rows)
        query_block = lax.dynamic_slice_in_dim(query, query_start, QB, 0)
        key_block = lax.dynamic_slice_in_dim(keys, key_start, 5 * QB, 0)
        value_block = lax.dynamic_slice_in_dim(values, key_start, 5 * QB, 0)
        scores = masked_scores(query_block, key_block, segment, query_start, key_start)
        highest = jnp.max(scores, axis=2, keepdims=True)
        weights = jnp.exp(scores - highest)
        totals = jnp.sum(weights, axis=2, keepdims=True)
        softmax_rows = (weights / totals).astype(jnp.bfloat16)
        mixed = jnp.einsum(
            "hqk,khd->qhd", softmax_rows, value_block, preferred_element_type=jnp.float32
        )
        return (mixed.astype(jnp.bfloat16), (highest + jnp.log(totals))[:, :, 0])

    return lax.map(one_block, jnp.arange(total_rows // QB, dtype=jnp.int32))


def attention_backward(query, keys, values, mixed_grad, logsum, segment):
    total_rows, heads_local, head_size = query.shape

    def one_block(carry, block_index):
        key_total, value_total = carry
        query_start, key_start = block_window(block_index, total_rows)
        query_block = lax.dynamic_slice_in_dim(query, query_start, QB, 0)
        key_block = lax.dynamic_slice_in_dim(keys, key_start, 5 * QB, 0)
        value_block = lax.dynamic_slice_in_dim(values, key_start, 5 * QB, 0)
        grad_block = lax.dynamic_slice_in_dim(mixed_grad, query_start, QB, 0)
        scores = masked_scores(query_block, key_block, segment, query_start, key_start)
        softmax_full = jnp.exp(scores - logsum[block_index][:, :, None])
        softmax_rows = softmax_full.astype(jnp.bfloat16)
        weight_grad = jnp.einsum(
            "qhd,khd->hqk", grad_block, value_block, preferred_element_type=jnp.float32
        )
        row_dot = jnp.sum(softmax_full * weight_grad, axis=2, keepdims=True)
        score_grad = (softmax_full * (weight_grad - row_dot)).astype(jnp.bfloat16)
        query_grad = (
            jnp.einsum("hqk,khd->qhd", score_grad, key_block, preferred_element_type=jnp.float32)
            * 0.125
        ).astype(jnp.bfloat16)
        key_part = (
            jnp.einsum("hqk,qhd->khd", score_grad, query_block, preferred_element_type=jnp.float32)
            * 0.125
        )
        value_part = jnp.einsum(
            "hqk,qhd->khd", softmax_rows, grad_block, preferred_element_type=jnp.float32
        )
        key_total = lax.dynamic_update_slice_in_dim(
            key_total,
            lax.dynamic_slice_in_dim(key_total, key_start, 5 * QB, 0) + key_part,
            key_start,
            0,
        )
        value_total = lax.dynamic_update_slice_in_dim(
            value_total,
            lax.dynamic_slice_in_dim(value_total, key_start, 5 * QB, 0) + value_part,
            key_start,
            0,
        )
        return ((key_total, value_total), query_grad)

    empty = jnp.zeros((total_rows, heads_local, head_size), jnp.float32)
    (key_total, value_total), query_grad = lax.scan(
        one_block, (empty, empty), jnp.arange(total_rows // QB, dtype=jnp.int32)
    )
    flat = (total_rows, heads_local * head_size)
    return (
        query_grad.reshape(flat),
        key_total.astype(jnp.bfloat16).reshape(flat),
        value_total.astype(jnp.bfloat16).reshape(flat),
    )


def per_device(
    pixels,
    embed_weight,
    embed_bias,
    first_gain,
    first_shift,
    query_weight,
    query_bias,
    key_weight,
    value_weight,
    value_bias,
    output_weight,
    output_bias,
    second_gain,
    second_shift,
    up_weight,
    up_bias,
    down_weight,
    down_bias,
    cotangent,
    item_lengths,
    item_kind,
    sampling_level,
):
    tensor_size = lax.axis_size("mp")
    local_rows = pixels.shape[0]
    model_width = embed_bias.shape[1]
    group_rows = local_rows * tensor_size
    used_rows = group_rows - min(group_rows // 64, ITEM_MAX)
    local_width = query_weight.shape[1]
    heads_local = local_width // HD
    row_start = lax.axis_index("mp") * local_rows
    all_rows = jnp.arange(group_rows, dtype=jnp.int32)
    segment, offset_all, band_all, level_all = row_tables(
        item_lengths[0], item_kind[0], sampling_level[0], all_rows, used_rows, GRID
    )
    offset = lax.dynamic_slice_in_dim(offset_all, row_start, local_rows, 0)
    band = lax.dynamic_slice_in_dim(band_all, row_start, local_rows, 0)
    level = lax.dynamic_slice_in_dim(level_all, row_start, local_rows, 0)
    band_hot = (band[:, None] == jnp.arange(embed_bias.shape[0], dtype=jnp.int32)[None, :]).astype(
        jnp.float32
    )
    code = position_code(offset, level, model_width, GRID)
    full_embed = lax.all_gather(embed_weight, "mp", axis=2, tiled=True)
    flat_embed = full_embed.reshape(-1, model_width)
    expanded = (band_hot.astype(jnp.bfloat16)[:, :, None] * pixels[:, None, :]).reshape(
        local_rows, -1
    )
    embedded = jnp.dot(expanded, flat_embed, preferred_element_type=jnp.float32)
    start = (
        embedded
        + jnp.dot(band_hot, embed_bias.astype(jnp.float32), precision=HIGHEST_PRECISION)
        + code
    )
    normed1, scaled1, inverse1 = norm_parts(start, first_gain, first_shift)
    gathered1 = lax.all_gather(normed1, "mp", axis=0, tiled=True)
    merged_weight = jnp.concatenate([query_weight, key_weight, value_weight], axis=1)
    merged_bias = jnp.concatenate(
        [
            query_bias.astype(jnp.float32),
            jnp.zeros((local_width,), jnp.float32),
            value_bias.astype(jnp.float32),
        ]
    )
    projected = (
        jnp.dot(gathered1, merged_weight, preferred_element_type=jnp.float32) + merged_bias
    ).astype(jnp.bfloat16)
    shaped = (group_rows, heads_local, HD)
    query = projected[:, :local_width].reshape(shaped)
    keys = projected[:, local_width : 2 * local_width].reshape(shaped)
    values = projected[:, 2 * local_width :].reshape(shaped)
    attended, logsum = attention_forward(query, keys, values, segment)
    attended = attended.reshape(group_rows, local_width)
    rows = attended
    branch = lax.psum_scatter(
        jnp.dot(rows, output_weight, preferred_element_type=jnp.float32).astype(jnp.bfloat16),
        "mp",
        scatter_dimension=0,
        tiled=True,
    ).astype(jnp.float32)
    middle = start + branch + output_bias
    normed2, scaled2, inverse2 = norm_parts(middle, second_gain, second_shift)
    gathered2 = lax.all_gather(normed2, "mp", axis=0, tiled=True)
    hidden = jnp.dot(gathered2, up_weight, preferred_element_type=jnp.float32) + up_bias
    activated = jax.nn.gelu(hidden, approximate=False).astype(jnp.bfloat16)
    rows = activated
    mlp_branch = lax.psum_scatter(
        jnp.dot(rows, down_weight, preferred_element_type=jnp.float32).astype(jnp.bfloat16),
        "mp",
        scatter_dimension=0,
        tiled=True,
    ).astype(jnp.float32)
    final = middle + mlp_branch + down_bias
    layer_output = final.astype(jnp.bfloat16)
    own_rows = row_start + jnp.arange(local_rows, dtype=jnp.int32)
    valid = (own_rows < used_rows).astype(jnp.float32)[:, None]
    upstream = cotangent.astype(jnp.float32) * valid
    down_bias_grad = jnp.sum(upstream, axis=0)
    upstream_low = upstream.astype(jnp.bfloat16)
    gathered_grad = lax.all_gather(upstream_low, "mp", axis=0, tiled=True)
    down_weight_grad = jnp.dot(activated.T, gathered_grad, preferred_element_type=jnp.float32)
    hidden_grad = (
        jnp.dot(gathered_grad, down_weight.T, preferred_element_type=jnp.float32)
        * gelu_slope(hidden)
    ).astype(jnp.bfloat16)
    up_bias_grad = jnp.sum(hidden_grad, axis=0, dtype=jnp.float32)
    up_weight_grad = jnp.dot(gathered2.T, hidden_grad, preferred_element_type=jnp.float32)
    rows = hidden_grad
    normed2_grad = lax.psum_scatter(
        jnp.dot(rows, up_weight.T, preferred_element_type=jnp.float32).astype(jnp.bfloat16),
        "mp",
        scatter_dimension=0,
        tiled=True,
    ).astype(jnp.float32)
    second_gain_grad = jnp.sum(normed2_grad * scaled2, axis=0)
    second_shift_grad = jnp.sum(normed2_grad, axis=0)
    middle_grad = upstream + norm_back(normed2_grad, scaled2, inverse2, second_gain)
    output_bias_grad = jnp.sum(middle_grad, axis=0)
    middle_low = middle_grad.astype(jnp.bfloat16)
    gathered_middle = lax.all_gather(middle_low, "mp", axis=0, tiled=True)
    output_weight_grad = jnp.dot(attended.T, gathered_middle, preferred_element_type=jnp.float32)
    mixed_grad = jnp.dot(
        gathered_middle, output_weight.T, preferred_element_type=jnp.float32
    ).astype(jnp.bfloat16)
    query_grad, key_grad, value_grad = attention_backward(
        query, keys, values, mixed_grad.reshape(shaped), logsum, segment
    )
    query_bias_grad = jnp.sum(query_grad, axis=0, dtype=jnp.float32)
    value_bias_grad = jnp.sum(value_grad, axis=0, dtype=jnp.float32)
    merged_grad = jnp.concatenate([query_grad, key_grad, value_grad], axis=1)
    merged_weight_grad = jnp.dot(gathered1.T, merged_grad, preferred_element_type=jnp.float32)
    query_weight_part = merged_weight_grad[:, :local_width]
    key_weight_part = merged_weight_grad[:, local_width : 2 * local_width]
    value_weight_part = merged_weight_grad[:, 2 * local_width :]
    rows = merged_grad
    normed1_grad = lax.psum_scatter(
        jnp.dot(rows, merged_weight.T, preferred_element_type=jnp.float32).astype(jnp.bfloat16),
        "mp",
        scatter_dimension=0,
        tiled=True,
    ).astype(jnp.float32)
    first_gain_grad = jnp.sum(normed1_grad * scaled1, axis=0)
    first_shift_grad = jnp.sum(normed1_grad, axis=0)
    start_grad = middle_grad + norm_back(normed1_grad, scaled1, inverse1, first_gain)
    start_low = start_grad.astype(jnp.bfloat16)
    spread_grad = jnp.dot(start_low, flat_embed.T, preferred_element_type=jnp.float32)
    pixel_gradient = jnp.sum(
        spread_grad.reshape(local_rows, band_hot.shape[1], -1) * band_hot[:, :, None], axis=1
    )
    embed_term = jnp.dot(expanded.T, start_low, preferred_element_type=jnp.float32).reshape(
        full_embed.shape
    )
    embed_weight_grad = lax.psum_scatter(
        embed_term.astype(jnp.bfloat16), "mp", scatter_dimension=2, tiled=True
    )
    embed_bias_grad = jnp.dot(band_hot.T, start_grad, precision=HIGHEST_PRECISION)
    (
        embed_weight_sum,
        query_weight_sum,
        query_bias_sum,
        key_weight_sum,
        value_weight_sum,
        value_bias_sum,
        output_weight_sum,
        up_weight_sum,
        up_bias_sum,
        down_weight_sum,
    ) = (
        lax.psum(embed_weight_grad, "dp").astype(jnp.float32),
        lax.psum(query_weight_part.astype(jnp.bfloat16), "dp").astype(jnp.float32),
        lax.psum(query_bias_grad.astype(jnp.bfloat16), "dp").astype(jnp.float32),
        lax.psum(key_weight_part.astype(jnp.bfloat16), "dp").astype(jnp.float32),
        lax.psum(value_weight_part.astype(jnp.bfloat16), "dp").astype(jnp.float32),
        lax.psum(value_bias_grad.astype(jnp.bfloat16), "dp").astype(jnp.float32),
        lax.psum(output_weight_grad.astype(jnp.bfloat16), "dp").astype(jnp.float32),
        lax.psum(up_weight_grad.astype(jnp.bfloat16), "dp").astype(jnp.float32),
        lax.psum(up_bias_grad.astype(jnp.bfloat16), "dp").astype(jnp.float32),
        lax.psum(down_weight_grad.astype(jnp.bfloat16), "dp").astype(jnp.float32),
    )
    (
        embed_bias_sum,
        first_gain_sum,
        first_shift_sum,
        output_bias_sum,
        second_gain_sum,
        second_shift_sum,
        down_bias_sum,
    ) = lax.psum(
        (
            embed_bias_grad,
            first_gain_grad,
            first_shift_grad,
            output_bias_grad,
            second_gain_grad,
            second_shift_grad,
            down_bias_grad,
        ),
        ("dp", "mp"),
    )
    return (
        layer_output,
        pixel_gradient,
        embed_weight_sum,
        embed_bias_sum,
        first_gain_sum,
        first_shift_sum,
        query_weight_sum,
        query_bias_sum,
        key_weight_sum,
        value_weight_sum,
        value_bias_sum,
        output_weight_sum,
        output_bias_sum,
        second_gain_sum,
        second_shift_sum,
        up_weight_sum,
        up_bias_sum,
        down_weight_sum,
        down_bias_sum,
    )


def solution(mesh):
    placed = (
        P(("dp", "mp"), None),
        P(None, None, "mp"),
        P(),
        P(),
        P(),
        P(None, "mp"),
        P("mp"),
        P(None, "mp"),
        P(None, "mp"),
        P("mp"),
        P("mp", None),
        P(),
        P(),
        P(),
        P(None, "mp"),
        P("mp"),
        P("mp", None),
        P(),
        P(("dp", "mp"), None),
        P("dp", None),
        P("dp", None),
        P("dp", None),
    )
    return jax.shard_map(
        per_device,
        mesh=mesh,
        in_specs=placed,
        out_specs=(
            P(("dp", "mp"), None),
            P(("dp", "mp"), None),
            P(None, None, "mp"),
            P(),
            P(),
            P(),
            P(None, "mp"),
            P("mp"),
            P(None, "mp"),
            P(None, "mp"),
            P("mp"),
            P("mp", None),
            P(),
            P(),
            P(),
            P(None, "mp"),
            P("mp"),
            P("mp", None),
            P(),
        ),
        check_vma=False,
    )
```

profile of v0, /device:TPU:0, one launch (start us, length us, event | category | flops | bytes accessed | tf_op | source)
XLA Modules:
  0.0 1496.7 jit_solution(3650666633741487799)
XLA Ops:
  19.5 64.5 %all-gather.6.cloned.1.call-done = bf16[4,1280,1024]{2,1,0:T(8,128)(2,1)} async-done(((bf16[4,1280,256]{2,1,0:T(8,128)(2,1)}), bf16[4,1280,1024]{2,1,0:T(8,128)(2,1)}) %all-gather.6.cloned.1.call-update) | async-done | bytes 10485776 | tf_op jit(solution)/shard_map/all_gather | solution.py:216
  101.9 36.8 %all-gather.8.cloned.1.call-done = bf16[2560,1024]{1,0:T(8,128)(2,1)} async-done(((bf16[640,1024]{1,0:T(8,128)(2,1)}), bf16[2560,1024]{1,0:T(8,128)(2,1)}) %all-gather.8.cloned.1.call-update) | async-done | bytes 5242896 | tf_op jit(solution)/shard_map/all_gather | solution.py:228
  148.9 155.1 %while.27 = (s32[]{:T(128)}, bf16[5,512,4,64]{1,3,2,0:T(8,128)(2,1)}, f32[5,4,512]{2,1,0:T(4,128)S(1)}, s32[5]{0:T(128)S(1)}, s32[2560]{0:T(1024)S(1)}, /*index=...) while((s32[]{:T(128)}, ...), condition=%wide.region_10.11_spmd, body=%wide.region_7.10_spmd.sunk | while | flops 1406531584 | bytes 155271392 | solution.py:115
  312.5 50.8 %reduce-scatter.6.cloned.1.call-done = bf16[640,1024]{1,0:T(8,128)(2,1)} async-done(((bf16[2560,1024]{1,0:T(8,128)(2,1)}), bf16[640,1024]{1,0:T(8,128)(2,1)}) %reduce-scatter.6.cloned.1.call-update) | async-done | bytes 1310736 | tf_op jit(solution)/shard_map/reduce_scatter | solution.py:247
  371.7 37.8 %all-gather.10.cloned.1.call-done = bf16[2560,1024]{1,0:T(8,128)(2,1)} async-done(((bf16[640,1024]{1,0:T(8,128)(2,1)}), bf16[2560,1024]{1,0:T(8,128)(2,1)}) %all-gather.10.cloned.1.call-update) | async-done | bytes 5242896 | tf_op jit(solution)/shard_map/all_gather | solution.py:255
  409.5 41.6 %fusion.40 = (bf16[2560,1024]{1,0:T(8,128)(2,1)}, f32[2560,1024]{1,0:T(8,128)}) fusion(f32[1024]{0:T(1024)S(1)} %convert_element_type.211, bf16[2560,1024]{1,0:T(8,128)(2,1)} %all-gather.10.cloned.1.call-done, bf16[1024,1024]{1,0:T(8,128)(2,1)S(1)} %copy-done), kind=kOutput, calls=%fused_computation.51 | convolution fusion | flops 5541724160 | bytes 23072768 | tf_op jit(solution)/shard_map/dot_general | solution.py:256
  487.0 39.4 %reduce-scatter.10.cloned.1.call-done = bf16[640,1024]{1,0:T(8,128)(2,1)} async-done(((bf16[2560,1024]{1,0:T(8,128)(2,1)}), bf16[640,1024]{1,0:T(8,128)(2,1)}) %reduce-scatter.10.cloned.1.call-update) | async-done | bytes 1310736 | tf_op jit(solution)/shard_map/reduce_scatter | solution.py:281
  530.4 50.0 %reduce-scatter.8.cloned.1.call-done = bf16[640,1024]{1,0:T(8,128)(2,1)} async-done(((bf16[2560,1024]{1,0:T(8,128)(2,1)}), bf16[640,1024]{1,0:T(8,128)(2,1)}) %reduce-scatter.8.cloned.1.call-update) | async-done | bytes 1310736 | tf_op jit(solution)/shard_map/reduce_scatter | solution.py:259
  588.0 40.5 %all-gather.14.cloned.1.call-done = bf16[2560,1024]{1,0:T(8,128)(2,1)} async-done(((bf16[640,1024]{1,0:T(8,128)(2,1)}), bf16[2560,1024]{1,0:T(8,128)(2,1)}) %all-gather.14.cloned.1.call-update) | async-done | bytes 5242896 | tf_op jit(solution)/shard_map/all_gather | solution.py:292
  634.8 379.1 %while.28 = (s32[]{:T(128)}, f32[2560,4,64]{0,2,1:T(8,128)}, f32[2560,4,64]{0,2,1:T(8,128)}, bf16[5,512,4,64]{1,3,2,0:T(8,128)(2,1)}, s32[5]{0:T(128)S(1)}, /*in...) while((s32[]{:T(128)}, f32[2560,4,64]{0,2,1:T(8,128)}, ...), condition=%wide.region_20.21_spmd.clone, body=%wide.region_18.20_spmd.clone.sunk | while | flops 3438934016 | bytes 225518000 | solution.py:162
  659.1 15.9 %multiply_reduce_fusion.5 = (f32[4,512]{1,0:T(4,128)S(1)}, f32[4,512,2560]{2,1,0:T(8,128)}) fusion(f32[4,512,2560]{2,1,0:T(8,128)} %fusion.171, f32[4,512]{1,0:T(4,128)S(1)} %dynamic-slice_bitcast_fusion.2, pred[512,2560]{1,0:T(8,128)(4,1)S(1)} %broadcast_compare_fusion.5, bf16[2560,4,64]{0,2,1:T(8,128)(2,1)S(1)} %copy-done.3, ...), kind=kOutput, calls=%fused_computation.17.clone.1 | convolution fusion | flops 697300992 | bytes 44843012 | tf_op jit(solution)/shard_map/while/body/eval_jaxpr/qhd,khd->hqk/dot_general | solution.py:131
  675.1 20.1 %multiply_convert_fusion.2 = bf16[4,512,2560]{2,1,0:T(8,128)(2,1)} fusion(f32[4,512,2560]{2,1,0:T(8,128)} %get-tuple-element.389, f32[4,512,2560]{2,1,0:T(8,128)} %fusion.171, f32[4,512]{1,0:T(4,128)S(1)} %get-tuple-element.390, f32[4,512]{1,0:T(4,128)S(1)} %dynamic-slice_bitcast_fusion.2, pred[512,2560]{1,0:T(8,128)(4,1)S(1)} %broadcast_compare_fusion.5), kind=kLoop, calls=%fused_computation.16.clone.1 | loop fusion | flops 31457280 | bytes 53755904 | tf_op jit(solution)/shard_map/while/body/eval_jaxpr/convert_element_type | solution.py:135
  734.9 15.9 %multiply_reduce_fusion.5 = (f32[4,512]{1,0:T(4,128)S(1)}, f32[4,512,2560]{2,1,0:T(8,128)}) fusion(f32[4,512,2560]{2,1,0:T(8,128)} %fusion.171, f32[4,512]{1,0:T(4,128)S(1)} %dynamic-slice_bitcast_fusion.2, pred[512,2560]{1,0:T(8,128)(4,1)S(1)} %broadcast_compare_fusion.5, bf16[2560,4,64]{0,2,1:T(8,128)(2,1)S(1)} %copy-done.3, ...), kind=kOutput, calls=%fused_computation.17.clone.1 | convolution fusion | flops 697300992 | bytes 44843012 | tf_op jit(solution)/shard_map/while/body/eval_jaxpr/qhd,khd->hqk/dot_general | solution.py:131
  750.8 20.1 %multiply_convert_fusion.2 = bf16[4,512,2560]{2,1,0:T(8,128)(2,1)} fusion(f32[4,512,2560]{2,1,0:T(8,128)} %get-tuple-element.389, f32[4,512,2560]{2,1,0:T(8,128)} %fusion.171, f32[4,512]{1,0:T(4,128)S(1)} %get-tuple-element.390, f32[4,512]{1,0:T(4,128)S(1)} %dynamic-slice_bitcast_fusion.2, pred[512,2560]{1,0:T(8,128)(4,1)S(1)} %broadcast_compare_fusion.5), kind=kLoop, calls=%fused_computation.16.clone.1 | loop fusion | flops 31457280 | bytes 53755904 | tf_op jit(solution)/shard_map/while/body/eval_jaxpr/convert_element_type | solution.py:135
  826.5 20.1 %multiply_convert_fusion.2 = bf16[4,512,2560]{2,1,0:T(8,128)(2,1)} fusion(f32[4,512,2560]{2,1,0:T(8,128)} %get-tuple-element.389, f32[4,512,2560]{2,1,0:T(8,128)} %fusion.171, f32[4,512]{1,0:T(4,128)S(1)} %get-tuple-element.390, f32[4,512]{1,0:T(4,128)S(1)} %dynamic-slice_bitcast_fusion.2, pred[512,2560]{1,0:T(8,128)(4,1)S(1)} %broadcast_compare_fusion.5), kind=kLoop, calls=%fused_computation.16.clone.1 | loop fusion | flops 31457280 | bytes 53755904 | tf_op jit(solution)/shard_map/while/body/eval_jaxpr/convert_element_type | solution.py:135
  886.3 15.9 %multiply_reduce_fusion.5 = (f32[4,512]{1,0:T(4,128)S(1)}, f32[4,512,2560]{2,1,0:T(8,128)}) fusion(f32[4,512,2560]{2,1,0:T(8,128)} %fusion.171, f32[4,512]{1,0:T(4,128)S(1)} %dynamic-slice_bitcast_fusion.2, pred[512,2560]{1,0:T(8,128)(4,1)S(1)} %broadcast_compare_fusion.5, bf16[2560,4,64]{0,2,1:T(8,128)(2,1)S(1)} %copy-done.3, ...), kind=kOutput, calls=%fused_computation.17.clone.1 | convolution fusion | flops 697300992 | bytes 44843012 | tf_op jit(solution)/shard_map/while/body/eval_jaxpr/qhd,khd->hqk/dot_general | solution.py:131
  902.2 20.1 %multiply_convert_fusion.2 = bf16[4,512,2560]{2,1,0:T(8,128)(2,1)} fusion(f32[4,512,2560]{2,1,0:T(8,128)} %get-tuple-element.389, f32[4,512,2560]{2,1,0:T(8,128)} %fusion.171, f32[4,512]{1,0:T(4,128)S(1)} %get-tuple-element.390, f32[4,512]{1,0:T(4,128)S(1)} %dynamic-slice_bitcast_fusion.2, pred[512,2560]{1,0:T(8,128)(4,1)S(1)} %broadcast_compare_fusion.5), kind=kLoop, calls=%fused_computation.16.clone.1 | loop fusion | flops 31457280 | bytes 53755904 | tf_op jit(solution)/shard_map/while/body/eval_jaxpr/convert_element_type | solution.py:135
  962.0 15.9 %multiply_reduce_fusion.5 = (f32[4,512]{1,0:T(4,128)S(1)}, f32[4,512,2560]{2,1,0:T(8,128)}) fusion(f32[4,512,2560]{2,1,0:T(8,128)} %fusion.171, f32[4,512]{1,0:T(4,128)S(1)} %dynamic-slice_bitcast_fusion.2, pred[512,2560]{1,0:T(8,128)(4,1)S(1)} %broadcast_compare_fusion.5, bf16[2560,4,64]{0,2,1:T(8,128)(2,1)S(1)} %copy-done.3, ...), kind=kOutput, calls=%fused_computation.17.clone.1 | convolution fusion | flops 697300992 | bytes 44843012 | tf_op jit(solution)/shard_map/while/body/eval_jaxpr/qhd,khd->hqk/dot_general | solution.py:131
  977.9 20.1 %multiply_convert_fusion.2 = bf16[4,512,2560]{2,1,0:T(8,128)(2,1)} fusion(f32[4,512,2560]{2,1,0:T(8,128)} %get-tuple-element.389, f32[4,512,2560]{2,1,0:T(8,128)} %fusion.171, f32[4,512]{1,0:T(4,128)S(1)} %get-tuple-element.390, f32[4,512]{1,0:T(4,128)S(1)} %dynamic-slice_bitcast_fusion.2, pred[512,2560]{1,0:T(8,128)(4,1)S(1)} %broadcast_compare_fusion.5), kind=kLoop, calls=%fused_computation.16.clone.1 | loop fusion | flops 31457280 | bytes 53755904 | tf_op jit(solution)/shard_map/while/body/eval_jaxpr/convert_element_type | solution.py:135
  1027.0 51.4 %reduce-scatter.12.cloned.1.call-done = bf16[640,1024]{1,0:T(8,128)(2,1)} async-done(((bf16[2560,1024]{1,0:T(8,128)(2,1)}), bf16[640,1024]{1,0:T(8,128)(2,1)}) %reduce-scatter.12.cloned.1.call-update) | async-done | bytes 1310736 | tf_op jit(solution)/shard_map/reduce_scatter | solution.py:308
  1128.5 53.4 %reduce-scatter.14.cloned.1.call-done = bf16[4,1280,256]{2,1,0:T(8,128)(2,1)} async-done(((bf16[4,1280,1024]{2,1,0:T(8,128)(2,1)}), bf16[4,1280,256]{2,1,0:T(8,128)(2,1)}) %reduce-scatter.14.cloned.1.call-update) | async-done | bytes 2621456 | tf_op jit(solution)/shard_map/reduce_scatter | solution.py:325
  1182.6 22.0 %all-reduce.1 = (bf16[256]{0:T(256)(128)(2,1)S(1)}, bf16[256]{0:T(256)(128)(2,1)S(1)}, bf16[1024]{0:T(1024)(128)(2,1)S(1)}) all-reduce(bf16[256]{0:T(256)(128)(2,1)S(1)} %reduce_sum.245, bf16[256]{0:T(256)(128)(2,1)S(1)} %reduce_sum.247, bf16[1024]{0:T(1024)(128)(2,1)S(1)} %copy-done.55), channel_id=1, replica_groups=mesh['dp'=8,'mp'=4] {'dp'}, use_global_device_ids=true, to_apply=%region_34.35 | all-reduce | flops 1536 | bytes 6144 | tf_op jit(solution)/shard_map/psum | solution.py:343
  1209.1 42.8 %all-reduce = (f32[4,1024]{1,0:T(4,128)}, f32[1024]{0:T(1024)}, f32[1024]{0:T(1024)}, f32[1024]{0:T(1024)}, f32[1024]{0:T(1024)}, /*index=5*/f32[1024]{0:T(1024)}, f32[1024]{0:T(1024)}) all-reduce(f32[4,1024]{1,0:T(4,128)S(1)} %fusion.83, f32[1024]{0:T(1024)S(1)} %get-tuple-element.164, ...), channel_id=1, replica_groups=mesh['dp'=8,'mp'=4] {'dp','mp'}, use_global_device_ids=true, to_apply=%region_27.28 | all-reduce | flops 10240 | bytes 81920 | tf_op jit(solution)/shard_map/psum | solution.py:360
  1264.5 209.8 %all-reduce.5.cloned.1.call-done = (bf16[4,1280,256]{2,1,0:T(8,128)(2,1)}, bf16[1024,256]{1,0:T(8,128)(2,1)}, bf16[1024,256]{1,0:T(8,128)(2,1)}, bf16[1024,256]{...) async-done(((bf16[4,1280,256]{2,1,0:T(8,128)(2,1)}, bf16[1024,256]{1,0:T(8,128)(2,1)}, ...) | async-done | bytes 8912912 | tf_op jit(solution)/shard_map/psum | solution.py:341
  (371 shorter events, 559.1 us)
Async XLA Ops:
  7.2 402.3 %copy-start = (bf16[1024,1024]{1,0:T(8,128)(2,1)S(1)}, bf16[1024,1024]{1,0:T(8,128)(2,1)}, u32[]{:S(2)}) copy-start(bf16[1024,1024]{1,0:T(8,128)(2,1)} %param.40) | copy-start | bytes 6291460
  7.2 76.7 %all-gather.6.cloned.1.call-start = ((), (), s32[]{:S(2)}) async-start(), calls=%async_computation.5 | async-start | bytes 13107200 | tf_op jit(solution)/shard_map/all_gather | solution.py:216
  8.0 130.7 %all-gather.8.cloned.1.call-start = ((), (), s32[]{:S(2)}) async-start(), calls=%async_computation.6 | async-start | bytes 6553600 | tf_op jit(solution)/shard_map/all_gather | solution.py:228
  12.9 81.3 %copy-start.35 = (s32[640]{0:T(1024)}, s32[640]{0:T(1024)S(1)}, u32[]{:S(2)}) copy-start(s32[640]{0:T(1024)S(1)} %fusion.87) | copy-start | bytes 7684
  13.7 80.6 %copy-start.48 = (bf16[640,4]{0,1:T(4,128)(2,1)}, bf16[640,4]{0,1:T(4,128)(2,1)S(1)}, u32[]{:S(2)}) copy-start(bf16[640,4]{0,1:T(4,128)(2,1)S(1)} %get-tuple-element.256) | copy-start | bytes 15364
  98.1 265.3 %reduce-scatter.6.cloned.1.call-start = ((), (), s32[]{:S(2)}) async-start(), calls=%async_computation.7 | async-start | bytes 6553600 | tf_op jit(solution)/shard_map/reduce_scatter | solution.py:247
  311.9 97.7 %all-gather.10.cloned.1.call-start = ((), (), s32[]{:S(2)}) async-start(), calls=%async_computation.8 | async-start | bytes 6553600 | tf_op jit(solution)/shard_map/all_gather | solution.py:255
  312.5 54.9 %copy-start.39 = (f32[1024]{0:T(1024)S(1)}, f32[1024]{0:T(1024)}, u32[]{:S(2)}) copy-start(f32[1024]{0:T(1024)} %param.38) | copy-start | bytes 12292
  312.5 54.9 %copy-start.51 = (f32[1024]{0:T(1024)S(1)}, f32[1024]{0:T(1024)}, u32[]{:S(2)}) copy-start(f32[1024]{0:T(1024)} %param.39) | copy-start | bytes 12292
  368.9 83.0 %all-gather.12.cloned.1.call-start = ((), (), s32[]{:S(2)}) async-start(), calls=%async_computation.10 | async-start | bytes 6553600 | tf_op jit(solution)/shard_map/all_gather | solution.py:272
  371.7 154.7 %reduce-scatter.10.cloned.1.call-start = ((), (), s32[]{:S(2)}) async-start(), calls=%async_computation.11 | async-start | bytes 6553600 | tf_op jit(solution)/shard_map/reduce_scatter | solution.py:281
  474.9 105.4 %reduce-scatter.8.cloned.1.call-start = ((), (), s32[]{:S(2)}) async-start(), calls=%async_computation.9 | async-start | bytes 6553600 | tf_op jit(solution)/shard_map/reduce_scatter | solution.py:259
  486.3 142.2 %all-gather.14.cloned.1.call-start = ((), (), s32[]{:S(2)}) async-start(), calls=%async_computation.12 | async-start | bytes 6553600 | tf_op jit(solution)/shard_map/all_gather | solution.py:292
  526.4 53.9 %copy-start.13 = (bf16[640,1024]{1,0:T(8,128)(2,1)S(1)}, bf16[640,1024]{1,0:T(8,128)(2,1)}, u32[]{:S(2)}) copy-start(bf16[640,1024]{1,0:T(8,128)(2,1)} %reduce-scatter.10.cloned.1.call-done) | copy-start | bytes 3932164
  585.1 43.4 %copy-start.29 = (bf16[256,1024]{1,0:T(8,128)(2,1)S(1)}, bf16[256,1024]{1,0:T(8,128)(2,1)}, u32[]{:S(2)}) copy-start(bf16[256,1024]{1,0:T(8,128)(2,1)} %param.36) | copy-start | bytes 1572868
  587.9 490.5 %reduce-scatter.12.cloned.1.call-start = ((), (), s32[]{:S(2)}) async-start(), calls=%async_computation.13 | async-start | bytes 6553600 | tf_op jit(solution)/shard_map/reduce_scatter | solution.py:308
  1026.9 51.5 %copy-start.34 = (f32[640]{0:T(1024)S(1)}, f32[640]{0:T(1024)}, u32[]{:S(2)}) copy-start(f32[640]{0:T(1024)} %copy-done.33) | copy-start | bytes 7684
  1026.9 51.5 %copy-start.38 = (f32[640]{0:T(1024)S(1)}, f32[640]{0:T(1024)}, u32[]{:S(2)}) copy-start(f32[640]{0:T(1024)} %copy-done.37) | copy-start | bytes 7684
  1026.9 51.5 %copy-start.41 = (f32[1024]{0:T(1024)S(1)}, f32[1024]{0:T(1024)}, u32[]{:S(2)}) copy-start(f32[1024]{0:T(1024)} %param.29) | copy-start | bytes 12292
  1027.0 155.0 %reduce-scatter.14.cloned.1.call-start = ((), (), s32[]{:S(2)}) async-start(), calls=%async_computation.14 | async-start | bytes 13107200 | tf_op jit(solution)/shard_map/reduce_scatter | solution.py:325
  1097.6 376.8 %all-reduce.5.cloned.1.call-start = ((), (), s32[]{:S(2)}) async-start(), calls=%async_computation.15 | async-start | bytes 17825792 | tf_op jit(solution)/shard_map/psum | solution.py:341
  1182.0 27.1 %copy-start.42 = (f32[1024]{0:T(1024)S(1)}, f32[1024]{0:T(1024)}, u32[]{:S(2)}) copy-start(f32[1024]{0:T(1024)} %get-tuple-element.162) | copy-start | bytes 12292
  1182.0 27.1 %copy-start.43 = (f32[1024]{0:T(1024)S(1)}, f32[1024]{0:T(1024)}, u32[]{:S(2)}) copy-start(f32[1024]{0:T(1024)} %get-tuple-element.168) | copy-start | bytes 12292
  1182.0 69.9 %copy-start.46 = (f32[640,4]{0,1:T(4,128)S(1)}, f32[640,4]{0,1:T(4,128)}, u32[]{:S(2)}) copy-start(f32[640,4]{0,1:T(4,128)} %get-tuple-element.255) | copy-start | bytes 30724
  (78 other events, 570.2 us)
Sparse Core Ops, SparseCore 0:
  9.6 74.2 all-gather.5
  98.2 40.4 all-gather.7
  312.0 51.3 reduce-scatter.5
  369.1 40.4 all-gather.9
  411.5 40.3 all-gather.11
  475.0 51.3 reduce-scatter.9
  528.9 51.3 reduce-scatter.7
  588.1 40.3 all-gather.13
  1027.1 51.3 reduce-scatter.11
  1097.7 84.2 reduce-scatter.13
  1188.5 285.8 all-reduce.4
where the time goes:
time: 1510 us; the launch traced here: 1500 us
  waiting for transfers between devices  636 us (42%)
  matrix products  492 us (33%)
  other arithmetic  191 us (13%)
  local copies, waits for them, and re-layouts  79.6 us (5%)
  blocking collectives  64.8 us (4%)
  loops' own time  17.5 us (1%)
    psum x1, waiting for transfers between devices, per_device(): lax.psum(embed_weight_grad, 'dp').astype(jnp.float32)  210 us
    convert_element_type x5, other arithmetic, one_block(): score_grad = (softmax_full * (weight_grad - row_dot)).astype(jnp.bfloat16)  100 us
    dot_general x5, matrix products, one_block(): jnp.einsum('qhd,khd->hqk', grad_block, value_block, preferred_element_typ...  79.7 us
    dot_general x10, matrix products, segment_scores(): jnp.einsum('qhd,khd->hqk', query_block, key_block, preferred_element_type...  73.9 us
    all_gather x1, waiting for transfers between devices, per_device(): full_embed = lax.all_gather(embed_weight, 'mp', axis=2, tiled=True)  64.5 us
    dot_general x5, matrix products, one_block(): jnp.einsum('hqk,khd->qhd', softmax_rows, value_block, preferred_element_t...  54.6 us
    reduce_scatter x1, waiting for transfers between devices, per_device(): lax.psum_scatter(embed_term.astype(jnp.bfloat16), 'mp', scatter_dimension...  53.4 us
    reduce_scatter x1, waiting for transfers between devices, per_device(): lax.psum_scatter(jnp.dot(rows, merged_weight.T, preferred_element_type=jn...  51.4 us
  transfers between devices with their start and end apart: 11, of which 11 were waited for; matrix products, arithmetic and copies ran while one was open for 8% of the time, Pallas kernels for 0%

commit v1 on v0

--- a/solution.py
+++ b/solution.py
@@ -3,12 +3,17 @@
 import jax
 import jax.numpy as jnp
 from jax import lax
+from jax.experimental import pallas as pl
+from jax.experimental.pallas import tpu as pltpu
 from jax.sharding import PartitionSpec as P
 
 HD = 64
 GRID = 14
-QB = 512
 ITEM_MAX = 588
+ALIGN = 16
+CHUNK = 128
+WINDOW = 640
+SCORE_SCALE = 0.125 * math.log2(math.e)
 
 
 HIGHEST_PRECISION = lax.Precision.HIGHEST
@@ -73,101 +78,202 @@
     )
 
 
-def block_window(block_index, total_rows):
-    query_start = block_index * QB
-    key_start = jnp.clip(query_start - 2 * QB, 0, total_rows - 5 * QB)
-    return (query_start, key_start)
-
-
-def segment_scores(query_block, key_block, query_segment, key_segment):
-    allowed = (query_segment[:, None] == key_segment[None, :])[None]
-    scores = (
-        jnp.einsum("qhd,khd->hqk", query_block, key_block, preferred_element_type=jnp.float32)
-        * 0.125
-    )
-    return jnp.where(allowed, scores, -1e30)
-
-
-def masked_scores(query_block, key_block, segment, query_start, key_start):
-    query_segment = lax.dynamic_slice_in_dim(segment, query_start, QB, 0)
-    key_segment = lax.dynamic_slice_in_dim(segment, key_start, 5 * QB, 0)
-    return segment_scores(query_block, key_block, query_segment, key_segment)
-
-
-def attention_forward(query, keys, values, segment):
-    total_rows = query.shape[0]
-
-    def one_block(block_index):
-        query_start, key_start = block_window(block_index, total_rows)
-        query_block = lax.dynamic_slice_in_dim(query, query_start, QB, 0)
-        key_block = lax.dynamic_slice_in_dim(keys, key_start, 5 * QB, 0)
-        value_block = lax.dynamic_slice_in_dim(values, key_start, 5 * QB, 0)
-        scores = masked_scores(query_block, key_block, segment, query_start, key_start)
-        highest = jnp.max(scores, axis=2, keepdims=True)
-        weights = jnp.exp(scores - highest)
-        totals = jnp.sum(weights, axis=2, keepdims=True)
-        softmax_rows = (weights / totals).astype(jnp.bfloat16)
-        mixed = jnp.einsum(
-            "hqk,khd->qhd", softmax_rows, value_block, preferred_element_type=jnp.float32
-        )
-        return (mixed.astype(jnp.bfloat16), (highest + jnp.log(totals))[:, :, 0])
-
-    return lax.map(one_block, jnp.arange(total_rows // QB, dtype=jnp.int32))
-
-
-def attention_backward(query, keys, values, mixed_grad, logsum, segment):
-    total_rows, heads_local, head_size = query.shape
-
-    def one_block(carry, block_index):
-        key_total, value_total = carry
-        query_start, key_start = block_window(block_index, total_rows)
-        query_block = lax.dynamic_slice_in_dim(query, query_start, QB, 0)
-        key_block = lax.dynamic_slice_in_dim(keys, key_start, 5 * QB, 0)
-        value_block = lax.dynamic_slice_in_dim(values, key_start, 5 * QB, 0)
-        grad_block = lax.dynamic_slice_in_dim(mixed_grad, query_start, QB, 0)
-        scores = masked_scores(query_block, key_block, segment, query_start, key_start)
-        softmax_full = jnp.exp(scores - logsum[block_index][:, :, None])
-        softmax_rows = softmax_full.astype(jnp.bfloat16)
-        weight_grad = jnp.einsum(
-            "qhd,khd->hqk", grad_block, value_block, preferred_element_type=jnp.float32
-        )
-        row_dot = jnp.sum(softmax_full * weight_grad, axis=2, keepdims=True)
-        score_grad = (softmax_full * (weight_grad - row_dot)).astype(jnp.bfloat16)
-        query_grad = (
-            jnp.einsum("hqk,khd->qhd", score_grad, key_block, preferred_element_type=jnp.float32)
-            * 0.125
-        ).astype(jnp.bfloat16)
-        key_part = (
-            jnp.einsum("hqk,qhd->khd", score_grad, query_block, preferred_element_type=jnp.float32)
-            * 0.125
-        )
-        value_part = jnp.einsum(
-            "hqk,qhd->khd", softmax_rows, grad_block, preferred_element_type=jnp.float32
-        )
-        key_total = lax.dynamic_update_slice_in_dim(
-            key_total,
-            lax.dynamic_slice_in_dim(key_total, key_start, 5 * QB, 0) + key_part,
-            key_start,
-            0,
-        )
-        value_total = lax.dynamic_update_slice_in_dim(
-            value_total,
-            lax.dynamic_slice_in_dim(value_total, key_start, 5 * QB, 0) + value_part,
-            key_start,
-            0,
-        )
-        return ((key_total, value_total), query_grad)
-
-    empty = jnp.zeros((total_rows, heads_local, head_size), jnp.float32)
-    (key_total, value_total), query_grad = lax.scan(
-        one_block, (empty, empty), jnp.arange(total_rows // QB, dtype=jnp.int32)
-    )
-    flat = (total_rows, heads_local * head_size)
-    return (
-        query_grad.reshape(flat),
-        key_total.astype(jnp.bfloat16).reshape(flat),
-        value_total.astype(jnp.bfloat16).reshape(flat),
-    )
+def item_table(lengths, used_rows, total_rows):
+    ends = jnp.cumsum(lengths, dtype=jnp.int32)
+    starts = jnp.concatenate([ends - lengths, jnp.full((1,), used_rows, jnp.int32)])
+    ends = jnp.concatenate([ends, jnp.full((1,), total_rows, jnp.int32)])
+    begin = jnp.minimum(starts // ALIGN * ALIGN, total_rows - WINDOW)
+    low = starts - begin
+    high = ends - begin
+    return jnp.stack([begin, low, high, (high + CHUNK - 1) // CHUNK])
+
+
+def head_masks():
+    lane = lax.broadcasted_iota(jnp.int32, (1, 2 * HD), 1)
+    first = lane < HD
+    return first, first.astype(jnp.bfloat16), (lane >= HD).astype(jnp.bfloat16)
+
+
+def two_heads(block, mask_a, mask_b):
+    return jnp.concatenate([block * mask_a, block * mask_b], axis=0)
+
+
+def product(left, right, left_dim, right_dim):
+    return lax.dot_general(
+        left,
+        right,
+        (((left_dim,), (right_dim,)), ((), ())),
+        preferred_element_type=jnp.float32,
+    )
+
+
+def forward_kernel(table, qkv_ref, out_ref, stat_ref):
+    first, mask_a, mask_b = head_masks()
+    pair = 2 * HD
+
+    def one_item(item, carry):
+        begin = pl.multiple_of(table[0, item], ALIGN)
+        low = table[1, item]
+        high = table[2, item]
+        keys = qkv_ref[pl.ds(begin, WINDOW), pair : 2 * pair]
+        values = qkv_ref[pl.ds(begin, WINDOW), 2 * pair : 3 * pair]
+        extended = jnp.concatenate([values, jnp.ones((WINDOW, pair), jnp.bfloat16)], axis=1)
+        place = lax.broadcasted_iota(jnp.int32, (1, WINDOW), 1)
+        bias = jnp.where((place >= low) & (place < high), 0.0, -1e30)
+
+        def one_chunk(chunk, inner):
+            rows = pl.ds(pl.multiple_of(begin + chunk * CHUNK, ALIGN), CHUNK)
+            stacked = two_heads(qkv_ref[rows, 0:pair], mask_a, mask_b)
+            scores = product(stacked, keys, 1, 1) * SCORE_SCALE + bias
+            highest = jnp.max(scores, axis=1, keepdims=True)
+            weights = jnp.exp2(scores - highest).astype(jnp.bfloat16)
+            sums = product(weights, extended, 1, 0)
+            mixed = jnp.where(first, sums[:CHUNK, :pair], sums[CHUNK:, :pair])
+            totals = jnp.where(first, sums[:CHUNK, pair:], sums[CHUNK:, pair:])
+            tops = jnp.where(first, highest[:CHUNK], highest[CHUNK:])
+            row = chunk * CHUNK + lax.broadcasted_iota(jnp.int32, (CHUNK, 1), 0)
+            keep = (row >= low) & (row < high)
+            out_ref[rows, :] = jnp.where(
+                keep, mixed / totals, out_ref[rows, :].astype(jnp.float32)
+            ).astype(jnp.bfloat16)
+            stat_ref[rows, :] = jnp.where(keep, tops + jnp.log2(totals), stat_ref[rows, :])
+            return inner
+
+        lax.fori_loop(0, table[3, item], one_chunk, 0)
+        return carry
+
+    lax.fori_loop(0, table.shape[1], one_item, 0)
+
+
+def backward_kernel(table, qkv_ref, grad_ref, stat_ref, out_ref, key_acc, value_acc):
+    first, mask_a, mask_b = head_masks()
+    pair = 2 * HD
+
+    def one_item(item, carry):
+        begin = pl.multiple_of(table[0, item], ALIGN)
+        low = table[1, item]
+        high = table[2, item]
+        window = pl.ds(begin, WINDOW)
+        keys = qkv_ref[window, pair : 2 * pair]
+        values = qkv_ref[window, 2 * pair : 3 * pair]
+        place = lax.broadcasted_iota(jnp.int32, (WINDOW, 1), 0)
+        inside = (place >= low) & (place < high)
+        bias = jnp.where(inside, 0.0, -1e30)
+        key_acc[...] = jnp.zeros_like(key_acc)
+        value_acc[...] = jnp.zeros_like(value_acc)
+
+        def one_chunk(chunk, inner):
+            rows = pl.ds(pl.multiple_of(begin + chunk * CHUNK, ALIGN), CHUNK)
+            query = two_heads(qkv_ref[rows, 0:pair], mask_a, mask_b)
+            grads = two_heads(grad_ref[rows, :], mask_a, mask_b)
+            turned = stat_ref[rows, :].T
+            stat = jnp.concatenate([turned[0:1], turned[HD : HD + 1]], axis=1)
+            spot = lax.broadcasted_iota(jnp.int32, (1, CHUNK), 1) + chunk * CHUNK
+            usable = (spot >= low) & (spot < high)
+            usable = jnp.concatenate([usable, usable], axis=1)
+            stat = jnp.where(usable, stat, 1e30)
+            probs = jnp.exp2(product(keys, query, 1, 1) * SCORE_SCALE + bias - stat)
+            slope = product(values, grads, 1, 1)
+            dots = jnp.sum(probs * slope, axis=0, keepdims=True)
+            score_grad = (probs * (slope - dots)).astype(jnp.bfloat16)
+            value_acc[...] += product(probs.astype(jnp.bfloat16), grads, 1, 0)
+            key_acc[...] += product(score_grad, query, 1, 0)
+            query_grad = product(score_grad, keys, 0, 0)
+            query_grad = jnp.where(first, query_grad[:CHUNK], query_grad[CHUNK:]) * 0.125
+            row = chunk * CHUNK + lax.broadcasted_iota(jnp.int32, (CHUNK, 1), 0)
+            keep = (row >= low) & (row < high)
+            out_ref[rows, 0:pair] = jnp.where(
+                keep, query_grad, out_ref[rows, 0:pair].astype(jnp.float32)
+            ).astype(jnp.bfloat16)
+            return inner
+
+        lax.fori_loop(0, table[3, item], one_chunk, 0)
+        for acc, spot, factor in ((key_acc, 1, 0.125), (value_acc, 2, 1.0)):
+            columns = slice(spot * pair, (spot + 1) * pair)
+            out_ref[window, columns] = jnp.where(
+                inside, acc[...] * factor, out_ref[window, columns].astype(jnp.float32)
+            ).astype(jnp.bfloat16)
+        return carry
+
+    lax.fori_loop(0, table.shape[1], one_item, 0)
+
+
+def attention_forward(projected, table):
+    total_rows, width = projected.shape
+    pair = 2 * HD
+    blocks = width // (3 * pair)
+    return pl.pallas_call(
+        forward_kernel,
+        out_shape=(
+            jax.ShapeDtypeStruct((total_rows, blocks * pair), jnp.bfloat16),
+            jax.ShapeDtypeStruct((total_rows, blocks * pair), jnp.float32),
+        ),
+        grid_spec=pltpu.PrefetchScalarGridSpec(
+            num_scalar_prefetch=1,
+            grid=(blocks,),
+            in_specs=[pl.BlockSpec((total_rows, 3 * pair), lambda h, _: (0, h))],
+            out_specs=(
+                pl.BlockSpec((total_rows, pair), lambda h, _: (0, h)),
+                pl.BlockSpec((total_rows, pair), lambda h, _: (0, h)),
+            ),
+        ),
+        cost_estimate=pl.CostEstimate(
+            flops=blocks * total_rows * WINDOW * 1024,
+            bytes_accessed=total_rows * width * 4,
+            transcendentals=blocks * total_rows * WINDOW * 2,
+        ),
+        name="attention_forward",
+    )(table, projected)
+
+
+def attention_backward(projected, mixed_grad, stat, table):
+    total_rows, width = projected.shape
+    pair = 2 * HD
+    blocks = width // (3 * pair)
+    return pl.pallas_call(
+        backward_kernel,
+        out_shape=jax.ShapeDtypeStruct((total_rows, width), jnp.bfloat16),
+        grid_spec=pltpu.PrefetchScalarGridSpec(
+            num_scalar_prefetch=1,
+            grid=(blocks,),
+            in_specs=[
+                pl.BlockSpec((total_rows, 3 * pair), lambda h, _: (0, h)),
+                pl.BlockSpec((total_rows, pair), lambda h, _: (0, h)),
+                pl.BlockSpec((total_rows, pair), lambda h, _: (0, h)),
+            ],
+            out_specs=pl.BlockSpec((total_rows, 3 * pair), lambda h, _: (0, h)),
+            scratch_shapes=[
+                pltpu.VMEM((WINDOW, pair), jnp.float32),
+                pltpu.VMEM((WINDOW, pair), jnp.float32),
+            ],
+        ),
+        cost_estimate=pl.CostEstimate(
+            flops=blocks * total_rows * WINDOW * 2560,
+            bytes_accessed=total_rows * width * 6,
+            transcendentals=blocks * total_rows * WINDOW * 2,
+        ),
+        name="attention_backward",
+    )(table, projected, mixed_grad, stat)
+
+
+def widen(part):
+    extra = -part.shape[-1] % (2 * HD)
+    return jnp.pad(part, [(0, 0)] * (part.ndim - 1) + [(0, extra)]) if extra else part
+
+
+def interleave(query_part, key_part, value_part):
+    pair = 2 * HD
+    query_part, key_part, value_part = widen(query_part), widen(key_part), widen(value_part)
+    lead = query_part.shape[:-1]
+    parts = [part.reshape(*lead, -1, 1, pair) for part in (query_part, key_part, value_part)]
+    return jnp.concatenate(parts, axis=-2).reshape(*lead, -1)
+
+
+def separate(merged, width):
+    pair = 2 * HD
+    lead = merged.shape[:-1]
+    split = merged.reshape(*lead, -1, 3, pair)
+    return [split[..., spot, :].reshape(*lead, -1)[..., :width] for spot in range(3)]
 
 
 def per_device(
@@ -200,7 +306,6 @@
     group_rows = local_rows * tensor_size
     used_rows = group_rows - min(group_rows // 64, ITEM_MAX)
     local_width = query_weight.shape[1]
-    heads_local = local_width // HD
     row_start = lax.axis_index("mp") * local_rows
     all_rows = jnp.arange(group_rows, dtype=jnp.int32)
     segment, offset_all, band_all, level_all = row_tables(
@@ -226,23 +331,18 @@
     )
     normed1, scaled1, inverse1 = norm_parts(start, first_gain, first_shift)
     gathered1 = lax.all_gather(normed1, "mp", axis=0, tiled=True)
-    merged_weight = jnp.concatenate([query_weight, key_weight, value_weight], axis=1)
-    merged_bias = jnp.concatenate(
-        [
-            query_bias.astype(jnp.float32),
-            jnp.zeros((local_width,), jnp.float32),
-            value_bias.astype(jnp.float32),
-        ]
+    merged_weight = interleave(query_weight, key_weight, value_weight)
+    merged_bias = interleave(
+        query_bias.astype(jnp.float32),
+        jnp.zeros((local_width,), jnp.float32),
+        value_bias.astype(jnp.float32),
     )
     projected = (
         jnp.dot(gathered1, merged_weight, preferred_element_type=jnp.float32) + merged_bias
     ).astype(jnp.bfloat16)
-    shaped = (group_rows, heads_local, HD)
-    query = projected[:, :local_width].reshape(shaped)
-    keys = projected[:, local_width : 2 * local_width].reshape(shaped)
-    values = projected[:, 2 * local_width :].reshape(shaped)
-    attended, logsum = attention_forward(query, keys, values, segment)
-    attended = attended.reshape(group_rows, local_width)
+    table = item_table(item_lengths[0], used_rows, group_rows)
+    attended, stat = attention_forward(projected, table)
+    attended = attended[:, :local_width]
     rows = attended
     branch = lax.psum_scatter(
         jnp.dot(rows, output_weight, preferred_element_type=jnp.float32).astype(jnp.bfloat16),
@@ -294,16 +394,11 @@
     mixed_grad = jnp.dot(
         gathered_middle, output_weight.T, preferred_element_type=jnp.float32
     ).astype(jnp.bfloat16)
-    query_grad, key_grad, value_grad = attention_backward(
-        query, keys, values, mixed_grad.reshape(shaped), logsum, segment
-    )
-    query_bias_grad = jnp.sum(query_grad, axis=0, dtype=jnp.float32)
-    value_bias_grad = jnp.sum(value_grad, axis=0, dtype=jnp.float32)
-    merged_grad = jnp.concatenate([query_grad, key_grad, value_grad], axis=1)
+    merged_grad = attention_backward(projected, widen(mixed_grad), stat, table)
+    merged_bias_grad = jnp.sum(merged_grad, axis=0, dtype=jnp.float32)
+    query_bias_grad, _, value_bias_grad = separate(merged_bias_grad, local_width)
     merged_weight_grad = jnp.dot(gathered1.T, merged_grad, preferred_element_type=jnp.float32)
-    query_weight_part = merged_weight_grad[:, :local_width]
-    key_weight_part = merged_weight_grad[:, local_width : 2 * local_width]
-    value_weight_part = merged_weight_grad[:, 2 * local_width :]
+    query_weight_part, key_weight_part, value_weight_part = separate(merged_weight_grad, local_width)
     rows = merged_grad
     normed1_grad = lax.psum_scatter(
         jnp.dot(rows, merged_weight.T, preferred_element_type=jnp.float32).astype(jnp.bfloat16),

time: 1510 us -> 1050 us (0.70)
  matrix products: 492 us -> 157 us
  other arithmetic: 191 us -> 54.2 us
  Pallas kernels: 0 us -> 98.5 us
  local copies, waits for them, and re-layouts: 79.6 us -> 20.9 us
  loops' own time: 17.5 us -> 0 us
    dot_general x35 -> x0, matrix products: 330 us -> none  [the longest x5 79.7 us: one_block(): jnp.einsum('qhd,khd->hqk', grad_block, value_block, preferred_element_typ...]
    convert_element_type x8 -> x0, other arithmetic: 102 us -> none  [the longest x5 100 us: one_block(): score_grad = (softmax_full * (weight_grad - row_dot)).astype(jnp.bfloat16)]
    pallas_call x0 -> x2, Pallas kernels: none -> 98.5 us  [the longest x1 52.2 us: attention_backward(): pl.pallas_call(backward_kernel, out_shape=jax.ShapeDtypeStruct((total_row...]
    while x62 -> x0, local copies, waits for them, and re-layouts: 45.5 us -> none
    reduce_sum x7 -> x1, other arithmetic: 29.3 us -> 2.75 us  [per_device(): merged_bias_grad = jnp.sum(merged_grad, axis=0, dtype=jnp.float32)]
    another operation x2 -> x0, loops' own time: 17.5 us -> none  [the longest x1 13.8 us: attention_backward(): lax.scan(one_block, (empty, empty), jnp.arange(total_rows // QB, dtype=jn...]
  transfers between devices with their start and end apart: 11 -> 11, of which waited for: 11 -> 11; matrix products, arithmetic and copies ran while one was open for 8% -> 11% of each run, Pallas kernels for 0% -> 0%
where the time goes in v1:
time: 1050 us
  waiting for transfers between devices  635 us (60%)
  matrix products  157 us (15%)
  Pallas kernels  98.5 us (9%)
  blocking collectives  64.7 us (6%)
  other arithmetic  54.2 us (5%)
  local copies, waits for them, and re-layouts  20.9 us (2%)
  between operations  14.9 us (1%)
    psum x1, waiting for transfers between devices, per_device(): lax.psum(embed_weight_grad, 'dp').astype(jnp.float32)  208 us
    all_gather x1, waiting for transfers between devices, per_device(): full_embed = lax.all_gather(embed_weight, 'mp', axis=2, tiled=True)  64.5 us
    pallas_call x1, Pallas kernels, attention_backward(): pl.pallas_call(backward_kernel, out_shape=jax.ShapeDtypeStruct((total_row...  52.2 us
    reduce_scatter x1, waiting for transfers between devices, per_device(): lax.psum_scatter(jnp.dot(rows, down_weight, preferred_element_type=jnp.fl...  50.6 us
    reduce_scatter x1, waiting for transfers between devices, per_device(): lax.psum_scatter(jnp.dot(rows, merged_weight.T, preferred_element_type=jn...  50 us
    reduce_scatter x1, waiting for transfers between devices, per_device(): lax.psum_scatter(jnp.dot(rows, output_weight, preferred_element_type=jnp....  49.4 us
    reduce_scatter x1, waiting for transfers between devices, per_device(): lax.psum_scatter(embed_term.astype(jnp.bfloat16), 'mp', scatter_dimension...  48.9 us
    pallas_call x1, Pallas kernels, attention_forward(): pl.pallas_call(forward_kernel, out_shape=(jax.ShapeDtypeStruct((total_row...  46.3 us
  transfers between devices with their start and end apart: 11, of which 11 were waited for; matrix products, arithmetic and copies ran while one was open for 11% of the time, Pallas kernels for 0%

profile of v1, /device:TPU:0, one launch (start us, length us, event | category | flops | bytes accessed | tf_op | source)
XLA Modules:
  0.0 1046.6 jit_solution(12120284016663430351)
XLA Ops:
  19.5 64.5 %all-gather.6.cloned.1.call-done = bf16[4,1280,1024]{2,1,0:T(8,128)(2,1)} async-done(((bf16[4,1280,256]{2,1,0:T(8,128)(2,1)}), bf16[4,1280,1024]{2,1,0:T(8,128)(2,1)}) %all-gather.6.cloned.1.call-update) | async-done | bytes 10485776 | tf_op jit(solution)/shard_map/all_gather | solution.py:321
  83.9 10.3 fusion.16
  105.8 33.4 %all-gather.8.cloned.1.call-done = bf16[2560,1024]{1,0:T(8,128)(2,1)} async-done(((bf16[640,1024]{1,0:T(8,128)(2,1)}), bf16[2560,1024]{1,0:T(8,128)(2,1)}) %all-gather.8.cloned.1.call-update) | async-done | bytes 5242896 | tf_op jit(solution)/shard_map/all_gather | solution.py:333
  139.2 9.2 add_convert_fusion.qkv_ref
  148.4 46.3 %attention_forward.1 = (bf16[2560,256]{1,0:T(8,128)(2,1)}, f32[2560,256]{1,0:T(8,128)}) custom-call(s32[4,6]{1,0:T(4,128)} %pad_add_fusion.table, bf16[2560,768]{1,0:T(8,128)(2,1)} %add_convert_fusion.qkv_ref), custom_call_target="tpu_custom_call" | custom-call | flops 3355443200 | bytes 7864320 | tf_op jit(solution)/shard_map/attention_forward/pallas_call | solution.py:205
  200.6 49.4 %reduce-scatter.6.cloned.1.call-done = bf16[640,1024]{1,0:T(8,128)(2,1)} async-done(((bf16[2560,1024]{1,0:T(8,128)(2,1)}), bf16[640,1024]{1,0:T(8,128)(2,1)}) %reduce-scatter.6.cloned.1.call-update) | async-done | bytes 1310736 | tf_op jit(solution)/shard_map/reduce_scatter | solution.py:347
  257.6 38.6 %all-gather.10.cloned.1.call-done = bf16[2560,1024]{1,0:T(8,128)(2,1)} async-done(((bf16[640,1024]{1,0:T(8,128)(2,1)}), bf16[2560,1024]{1,0:T(8,128)(2,1)}) %all-gather.10.cloned.1.call-update) | async-done | bytes 5242896 | tf_op jit(solution)/shard_map/all_gather | solution.py:355
  296.2 30.4 %fusion.2 = (bf16[2560,1024]{1,0:T(8,128)(2,1)}, f32[2560,1024]{1,0:T(8,128)}) fusion(f32[1024]{0:T(1024)S(1)} %convert_element_type.194, bf16[2560,1024]{1,0:T(8,128)(2,1)} %all-gather.10.cloned.1.call-done, bf16[1024,1024]{1,0:T(8,128)(2,1)S(1)} %copy-done), kind=kOutput, calls=%fused_computation.6 | convolution fusion | flops 5541724160 | bytes 23072768 | tf_op jit(solution)/shard_map/dot_general | solution.py:356
  326.6 11.4 %all-gather.12.cloned.1.call-done = bf16[2560,1024]{1,0:T(8,128)(2,1)} async-done(((bf16[640,1024]{1,0:T(8,128)(2,1)}), bf16[2560,1024]{1,0:T(8,128)(2,1)}) %all-gather.12.cloned.1.call-update) | async-done | bytes 5242896 | tf_op jit(solution)/shard_map/all_gather | solution.py:372
  338.0 12.4 %fusion.64 = (bf16[1024]{0:T(1024)(128)(2,1)S(1)}, bf16[2560,1024]{1,0:T(8,128)(2,1)S(1)}) fusion(f32[2560,1024]{1,0:T(8,128)} %get-tuple-element.82, f32[1024]{0:T(1024)S(1)} %convert_element_type.194, bf16[2560,1024]{1,0:T(8,128)(2,1)} %all-gather.12.cloned.1.call-done, bf16[1024,1024]{1,0:T(8,128)(2,1)} %param.38), kind=kOutput, calls=%fused_computation.160 | convolution fusion | flops 5400165376 | bytes 23074816 | tf_op jit(solution)/shard_map/dot_general | solution.py:375
  361.9 9.8 convolution_convert_fusion.4
  372.4 39.4 %reduce-scatter.10.cloned.1.call-done = bf16[640,1024]{1,0:T(8,128)(2,1)} async-done(((bf16[2560,1024]{1,0:T(8,128)(2,1)}), bf16[640,1024]{1,0:T(8,128)(2,1)}) %reduce-scatter.10.cloned.1.call-update) | async-done | bytes 1310736 | tf_op jit(solution)/shard_map/reduce_scatter | solution.py:381
  415.2 50.6 %reduce-scatter.8.cloned.1.call-done = bf16[640,1024]{1,0:T(8,128)(2,1)} async-done(((bf16[2560,1024]{1,0:T(8,128)(2,1)}), bf16[640,1024]{1,0:T(8,128)(2,1)}) %reduce-scatter.8.cloned.1.call-update) | async-done | bytes 1310736 | tf_op jit(solution)/shard_map/reduce_scatter | solution.py:359
  472.5 40.5 %all-gather.14.cloned.1.call-done = bf16[2560,1024]{1,0:T(8,128)(2,1)} async-done(((bf16[640,1024]{1,0:T(8,128)(2,1)}), bf16[2560,1024]{1,0:T(8,128)(2,1)}) %all-gather.14.cloned.1.call-update) | async-done | bytes 5242896 | tf_op jit(solution)/shard_map/all_gather | solution.py:392
  518.1 52.2 %attention_backward.1 = bf16[2560,768]{1,0:T(8,128)(2,1)} custom-call(s32[4,6]{1,0:T(4,128)} %pad_add_fusion.table, bf16[2560,768]{1,0:T(8,128)(2,1)} %add_convert_fusion.qkv_ref, bf16[2560,256]{1,0:T(8,128)(2,1)} %convolution_convert_fusion.5.grad_ref, f32[2560,256]{1,0:T(8,128)} %get-tuple-element.22.stat_ref), custom_call_target="tpu_custom_call" | custom-call | flops 8388608000 | bytes 11796480 | tf_op jit(solution)/shard_map/attention_backward/pallas_call | solution.py:233
  578.5 50.0 %reduce-scatter.12.cloned.1.call-done = bf16[640,1024]{1,0:T(8,128)(2,1)} async-done(((bf16[2560,1024]{1,0:T(8,128)(2,1)}), bf16[640,1024]{1,0:T(8,128)(2,1)}) %reduce-scatter.12.cloned.1.call-update) | async-done | bytes 1310736 | tf_op jit(solution)/shard_map/reduce_scatter | solution.py:403
  636.9 10.6 %convolution_convert_fusion = bf16[4,1280,1024]{2,1,0:T(8,128)(2,1)} fusion(bf16[640,1280]{0,1:T(8,128)(2,1)S(1)} %copy-done.16, bf16[640,4]{0,1:T(4,128)(2,1)S(1)} %copy-done.34, f32[640,1024]{1,0:T(8,128)S(1)} %fusion.30), kind=kOutput, calls=%fused_computation.2 | convolution fusion | flops 6720061440 | bytes 14750720 | tf_op jit(solution)/shard_map/dot_general | solution.py:417
  647.9 10.3 convolution_convert_fusion.6
  658.1 12.5 %convolution_convert_fusion.7 = bf16[1024,1024]{1,0:T(8,128)(2,1)} fusion(bf16[2560,1024]{1,0:T(8,128)(2,1)} %all-gather.10.cloned.1.call-done, bf16[2560,1024]{1,0:T(8,128)(2,1)} %copy-done.46), kind=kOutput, calls=%fused_computation.77 | convolution fusion | flops 5369757696 | bytes 12582912 | tf_op jit(solution)/shard_map/dot_general | solution.py:379
  683.1 48.9 %reduce-scatter.14.cloned.1.call-done = bf16[4,1280,256]{2,1,0:T(8,128)(2,1)} async-done(((bf16[4,1280,1024]{2,1,0:T(8,128)(2,1)}), bf16[4,1280,256]{2,1,0:T(8,128)(2,1)}) %reduce-scatter.14.cloned.1.call-update) | async-done | bytes 2621456 | tf_op jit(solution)/shard_map/reduce_scatter | solution.py:420
  734.8 22.4 %all-reduce.1 = (bf16[256]{0:T(256)(128)(2,1)S(1)}, bf16[256]{0:T(256)(128)(2,1)S(1)}, bf16[1024]{0:T(1024)(128)(2,1)S(1)}) all-reduce(bf16[256]{0:T(256)(128)(2,1)S(1)} %bitcast.78, bf16[256]{0:T(256)(128)(2,1)S(1)} %bitcast.77, bf16[1024]{0:T(1024)(128)(2,1)S(1)} %get-tuple-element.83), channel_id=1, replica_groups=mesh['dp'=8,'mp'=4] {'dp'}, use_global_device_ids=true, to_apply=%region_27.28 | all-reduce | flops 1536 | bytes 6144 | tf_op jit(solution)/shard_map/psum | solution.py:438
  761.6 42.3 %all-reduce = (f32[4,1024]{1,0:T(4,128)}, f32[1024]{0:T(1024)}, f32[1024]{0:T(1024)}, f32[1024]{0:T(1024)}, f32[1024]{0:T(1024)}, /*index=5*/f32[1024]{0:T(1024)}, f32[1024]{0:T(1024)}) all-reduce(f32[4,1024]{1,0:T(4,128)S(1)} %fusion.45, f32[1024]{0:T(1024)S(1)} %get-tuple-element.25, ...), channel_id=1, replica_groups=mesh['dp'=8,'mp'=4] {'dp','mp'}, use_global_device_ids=true, to_apply=%region_20.21 | all-reduce | flops 10240 | bytes 81920 | tf_op jit(solution)/shard_map/psum | solution.py:455
  803.9 12.6 %multiply_reduce_fusion = f32[640,1280]{1,0:T(8,128)} fusion(bf16[4,1280,1024]{2,1,0:T(8,128)(2,1)} %all-gather.6.cloned.1.call-done, f32[640,4]{0,1:T(4,128)S(1)} %copy-done.31, f32[640,1024]{1,0:T(8,128)} %copy-done.5), kind=kOutput, calls=%fused_computation.3 | convolution fusion | flops 6717276160 | bytes 16394240 | tf_op jit(solution)/shard_map/dot_general | solution.py:413
  816.6 207.6 %all-reduce.5.cloned.1.call-done = (bf16[4,1280,256]{2,1,0:T(8,128)(2,1)}, bf16[1024,256]{1,0:T(8,128)(2,1)}, bf16[1024,256]{1,0:T(8,128)(2,1)}, bf16[1024,256]{...) async-done(((bf16[4,1280,256]{2,1,0:T(8,128)(2,1)}, bf16[1024,256]{1,0:T(8,128)(2,1)}, ...) | async-done | bytes 8912912 | tf_op jit(solution)/shard_map/psum | solution.py:436
  (196 shorter events, 116.1 us)
Async XLA Ops:
  7.2 289.0 %copy-start = (bf16[1024,1024]{1,0:T(8,128)(2,1)S(1)}, bf16[1024,1024]{1,0:T(8,128)(2,1)}, u32[]{:S(2)}) copy-start(bf16[1024,1024]{1,0:T(8,128)(2,1)} %param.36) | copy-start | bytes 6291460
  7.2 76.7 %all-gather.6.cloned.1.call-start = ((), (), s32[]{:S(2)}) async-start(), calls=%async_computation.5 | async-start | bytes 13107200 | tf_op jit(solution)/shard_map/all_gather | solution.py:321
  8.0 131.3 %all-gather.8.cloned.1.call-start = ((), (), s32[]{:S(2)}) async-start(), calls=%async_computation.6 | async-start | bytes 6553600 | tf_op jit(solution)/shard_map/all_gather | solution.py:333
  12.9 81.3 %copy-start.24 = (s32[640]{0:T(1024)}, s32[640]{0:T(1024)S(1)}, u32[]{:S(2)}) copy-start(s32[640]{0:T(1024)S(1)} %fusion.49) | copy-start | bytes 7684
  13.7 80.6 %copy-start.33 = (bf16[640,4]{0,1:T(4,128)(2,1)}, bf16[640,4]{0,1:T(4,128)(2,1)S(1)}, u32[]{:S(2)}) copy-start(bf16[640,4]{0,1:T(4,128)(2,1)S(1)} %get-tuple-element.76) | copy-start | bytes 15364
  98.7 151.3 %reduce-scatter.6.cloned.1.call-start = ((), (), s32[]{:S(2)}) async-start(), calls=%async_computation.7 | async-start | bytes 6553600 | tf_op jit(solution)/shard_map/reduce_scatter | solution.py:347
  148.4 46.3 %copy-start.18 = (bf16[256,1024]{1,0:T(8,128)(2,1)S(1)}, bf16[256,1024]{1,0:T(8,128)(2,1)}, u32[]{:S(2)}) copy-start(bf16[256,1024]{1,0:T(8,128)(2,1)} %param.32) | copy-start | bytes 1572868
  199.9 96.2 %all-gather.10.cloned.1.call-start = ((), (), s32[]{:S(2)}) async-start(), calls=%async_computation.8 | async-start | bytes 6553600 | tf_op jit(solution)/shard_map/all_gather | solution.py:355
  200.6 53.4 %copy-start.28 = (f32[1024]{0:T(1024)S(1)}, f32[1024]{0:T(1024)}, u32[]{:S(2)}) copy-start(f32[1024]{0:T(1024)} %param.34) | copy-start | bytes 12292
  200.6 53.4 %copy-start.36 = (f32[1024]{0:T(1024)S(1)}, f32[1024]{0:T(1024)}, u32[]{:S(2)}) copy-start(f32[1024]{0:T(1024)} %param.35) | copy-start | bytes 12292
  255.6 82.4 %all-gather.12.cloned.1.call-start = ((), (), s32[]{:S(2)}) async-start(), calls=%async_computation.10 | async-start | bytes 6553600 | tf_op jit(solution)/shard_map/all_gather | solution.py:372
  257.1 154.7 %reduce-scatter.10.cloned.1.call-start = ((), (), s32[]{:S(2)}) async-start(), calls=%async_computation.11 | async-start | bytes 6553600 | tf_op jit(solution)/shard_map/reduce_scatter | solution.py:381
  360.3 105.4 %reduce-scatter.8.cloned.1.call-start = ((), (), s32[]{:S(2)}) async-start(), calls=%async_computation.9 | async-start | bytes 6553600 | tf_op jit(solution)/shard_map/reduce_scatter | solution.py:359
  371.7 141.3 %all-gather.14.cloned.1.call-start = ((), (), s32[]{:S(2)}) async-start(), calls=%async_computation.12 | async-start | bytes 6553600 | tf_op jit(solution)/shard_map/all_gather | solution.py:392
  411.8 53.9 %copy-start.6 = (bf16[640,1024]{1,0:T(8,128)(2,1)S(1)}, bf16[640,1024]{1,0:T(8,128)(2,1)}, u32[]{:S(2)}) copy-start(bf16[640,1024]{1,0:T(8,128)(2,1)} %reduce-scatter.10.cloned.1.call-done) | copy-start | bytes 3932164
  469.7 43.3 %copy-start.19 = (bf16[256,1024]{1,0:T(8,128)(2,1)S(1)}, bf16[256,1024]{1,0:T(8,128)(2,1)}, u32[]{:S(2)}) copy-start(bf16[256,1024]{1,0:T(8,128)(2,1)} %param.32) | copy-start | bytes 1572868
  472.4 156.1 %reduce-scatter.12.cloned.1.call-start = ((), (), s32[]{:S(2)}) async-start(), calls=%async_computation.13 | async-start | bytes 6553600 | tf_op jit(solution)/shard_map/reduce_scatter | solution.py:403
  518.1 52.2 %copy-start.17 = (bf16[1024,2,3,128]{0,3,2,1:T(8,128)(2,1)S(1)}, bf16[1024,2,3,128]{0,3,2,1:T(8,128)(2,1)}, u32[]{:S(2)}) copy-start(bf16[1024,2,3,128]{0,3,2,1:T(8,128)(2,1)} %pad_maximum_fusion) | copy-start | bytes 4718596
  578.4 50.1 %copy-start.23 = (f32[640]{0:T(1024)S(1)}, f32[640]{0:T(1024)}, u32[]{:S(2)}) copy-start(f32[640]{0:T(1024)} %copy-done.22) | copy-start | bytes 7684
  578.4 50.1 %copy-start.27 = (f32[640]{0:T(1024)S(1)}, f32[640]{0:T(1024)}, u32[]{:S(2)}) copy-start(f32[640]{0:T(1024)} %copy-done.26) | copy-start | bytes 7684
  578.4 50.1 %copy-start.30 = (f32[1024]{0:T(1024)S(1)}, f32[1024]{0:T(1024)}, u32[]{:S(2)}) copy-start(f32[1024]{0:T(1024)} %param.25) | copy-start | bytes 12292
  578.4 153.6 %reduce-scatter.14.cloned.1.call-start = ((), (), s32[]{:S(2)}) async-start(), calls=%async_computation.14 | async-start | bytes 13107200 | tf_op jit(solution)/shard_map/reduce_scatter | solution.py:420
  647.6 376.6 %all-reduce.5.cloned.1.call-start = ((), (), s32[]{:S(2)}) async-start(), calls=%async_computation.15 | async-start | bytes 17825792 | tf_op jit(solution)/shard_map/psum | solution.py:436
  732.0 71.9 %copy-start.31 = (f32[640,4]{0,1:T(4,128)S(1)}, f32[640,4]{0,1:T(4,128)}, u32[]{:S(2)}) copy-start(f32[640,4]{0,1:T(4,128)} %get-tuple-element.75) | copy-start | bytes 30724
  (36 other events, 199.7 us)
Sparse Core Ops, SparseCore 0:
  9.6 74.2 all-gather.5
  98.8 40.4 all-gather.7
  200.1 49.8 reduce-scatter.5
  255.7 40.4 all-gather.9
  297.6 40.3 all-gather.11
  360.4 51.3 reduce-scatter.9
  414.3 51.3 reduce-scatter.7
  472.5 40.4 all-gather.13
  578.5 49.9 reduce-scatter.11
  647.7 84.2 reduce-scatter.13
  738.5 285.6 all-reduce.4
